TPU v7x, 32 devices: a whole 2x2x4 slice. The times are simulated.
32 devices in a mesh: blk: 32 (over z, y, x, core).
Axes of the slice: x: 2, y: 2, z: 4, core: 2. Of those that a mesh axis runs over, the one named last changes fastest.
Arguments:
- adjacency: int32 [8192, 1280], P('blk'), may hold values 0 or 1
- weight: bfloat16 [8192, 1280], P('blk'), may hold values from -6 to 6
Outputs:
- closure: float32 [8192, 4352], P('blk')
All inputs are finite; a program needn't handle non-finite values. No bound on the sum of `adjacency` on one device may be relied on, other than what follows from the above.
Results may differ from a plain program's by a relative error of at most 0.0041.
Values may be sent and summed in bfloat16 or wider, within the bound.
A program may use at most 64 MiB of HBM per device.

v0:
```python
import math

import jax
import jax.numpy as jnp
from jax import lax
from jax.sharding import PartitionSpec as P

B = 512


def shifted(value, axis, steps):
    count = lax.axis_size(axis)
    pairs = [(source, (source + steps) % count) for source in range(count)]
    return lax.ppermute(value, axis, pairs)


def banded(adjacency, weight):
    row_count = adjacency.shape[0]
    reach = (adjacency.shape[1] // row_count - 1) // 2
    local_row = lax.broadcasted_iota(jnp.int32, adjacency.shape, 0)
    offset = lax.broadcasted_iota(jnp.int32, adjacency.shape, 1) - local_row - reach * row_count
    keep = (jnp.abs(offset) <= B) & ((adjacency == 1) | (offset == 0))
    return jnp.where(keep, weight, jnp.zeros_like(weight))


def neighbours(block_rows, reach):
    below = []
    above = []
    upward = block_rows
    downward = block_rows
    for hop_count in range(reach):
        upward = shifted(upward, "blk", -1)
        downward = shifted(downward, "blk", 1)
        above.append(upward)
        below.append(downward)
    return below[::-1] + [block_rows] + above


def combine(block_rows, others, scale):
    row_count = block_rows.shape[0]
    width_cols = block_rows.shape[1]
    reach = (width_cols // row_count - 1) // 2
    result = jnp.zeros((row_count, (4 * reach + 1) * row_count), jnp.float32)
    for column, neighbour in enumerate(others):
        begin_col = column * row_count
        product = jnp.dot(
            block_rows[:, begin_col : begin_col + row_count],
            neighbour,
            preferred_element_type=jnp.float32,
        )
        result = result.at[:, begin_col : begin_col + width_cols].add(product)
    return result * scale


def local(adjacency, weight):
    matrix = banded(adjacency, weight)
    row_count = matrix.shape[0]
    reach = (matrix.shape[1] // row_count - 1) // 2
    first_scale = 1.0 / math.sqrt(B)
    second_scale = 1.0 / math.sqrt(2 * B)
    stacked = neighbours(matrix, 3 * reach)
    squared_rows = []
    for index in range(4 * reach + 1):
        squared = combine(
            stacked[index + reach], stacked[index : index + 2 * reach + 1], first_scale
        )
        squared_rows.append(squared.astype(jnp.bfloat16))
    return combine(squared_rows[2 * reach], squared_rows, second_scale)


def solution(mesh):
    in_specs = (P("blk", None), P("blk", None))
    out_specs = P("blk", None)
    return jax.shard_map(local, mesh=mesh, in_specs=in_specs, out_specs=out_specs, check_vma=False)
```

profile of v0, /device:TPU:1, one launch (start us, length us, event | category | flops | bytes accessed | tf_op | source)
XLA Modules:
  0.0 131.7 jit_solution(6088994654334403607)
XLA Ops:
  0.0 1.9 %fusion.81 = bf16[256,1280]{1,0:T(8,128)(2,1)S(1)} fusion(bf16[256,1280]{1,0:T(8,128)(2,1)} %param.111, s32[256,1280]{1,0:T(8,128)} %param.110), kind=kLoop, calls=%fused_computation.147 | loop fusion | flops 2949120 | bytes 2621440 | tf_op jit(solution)/shard_map/jit(_where)/select_n | solution.py:23
  1.9 2.6 %collective-permute-start = (bf16[256,1280]{1,0:T(8,128)(2,1)S(1)}, bf16[256,1280]{1,0:T(8,128)(2,1)S(1)}, u32[]{:S(2)}, u32[]{:S(2)}) collective-permute-start(bf16[256,1280]{1,0:T(8,128)(2,1)S(1)} %fusion.81), channel_id=1, source_target_pairs={{0,1},{1,2},{2,3},{3,4},{4,5},{5,6},{6,7},{7,8},{8,9},{9,10},{10,1... | collective-permute-start | bytes 1966088 | tf_op jit(solution)/shard_map/ppermute | solution.py:14
  11.9 7.1 %collective-permute-done = bf16[256,1280]{1,0:T(8,128)(2,1)S(1)} collective-permute-done((bf16[256,1280]{1,0:T(8,128)(2,1)S(1)}, bf16[256,1280]{1,0:T(8,128)(2,1)S(1)}, u32[]{:S(2)}, u32[]{:S(2)}) %collective-permute-start) | collective-permute-done | bytes 655392 | tf_op jit(solution)/shard_map/ppermute | solution.py:14
  19.1 2.5 %collective-permute-start.1 = (bf16[256,1280]{1,0:T(8,128)(2,1)S(1)}, bf16[256,1280]{1,0:T(8,128)(2,1)S(1)}, u32[]{:S(2)}, u32[]{:S(2)}) collective-permute-start(bf16[256,1280]{1,0:T(8,128)(2,1)S(1)} %collective-permute-done), channel_id=1, source_target_pairs={{0,1},{1,2},{2,3},{3,4},{4,5},{5,6},{6,7},{7,8},{8,9},{9,10},{10,1... | collective-permute-start | bytes 1966088 | tf_op jit(solution)/shard_map/ppermute | solution.py:14
  24.9 11.2 %collective-permute-done.1 = bf16[256,1280]{1,0:T(8,128)(2,1)S(1)} collective-permute-done((bf16[256,1280]{1,0:T(8,128)(2,1)S(1)}, bf16[256,1280]{1,0:T(8,128)(2,1)S(1)}, u32[]{:S(2)}, u32[]{:S(2)}) %collective-permute-start.1) | collective-permute-done | bytes 655392 | tf_op jit(solution)/shard_map/ppermute | solution.py:14
  40.5 2.5 %collective-permute-start.4 = (bf16[256,1280]{1,0:T(8,128)(2,1)S(1)}, bf16[256,1280]{1,0:T(8,128)(2,1)S(1)}, u32[]{:S(2)}, u32[]{:S(2)}) collective-permute-start(bf16[256,1280]{1,0:T(8,128)(2,1)S(1)} %collective-permute-done.1), channel_id=1, source_target_pairs={{0,1},{1,2},{2,3},{3,4},{4,5},{5,6},{6,7},{7,8},{8,9},{9,10},{10,1... | collective-permute-start | bytes 1966088 | tf_op jit(solution)/shard_map/ppermute | solution.py:14
  43.0 1.2 fusion.71
  44.6 1.2 fusion.38
  48.1 8.7 %collective-permute-done.4 = bf16[256,1280]{1,0:T(8,128)(2,1)S(1)} collective-permute-done((bf16[256,1280]{1,0:T(8,128)(2,1)S(1)}, bf16[256,1280]{1,0:T(8,128)(2,1)S(1)}, u32[]{:S(2)}, u32[]{:S(2)}) %collective-permute-start.4) | collective-permute-done | bytes 655392 | tf_op jit(solution)/shard_map/ppermute | solution.py:14
  57.9 2.5 %collective-permute-start.5 = (bf16[256,1280]{1,0:T(8,128)(2,1)S(1)}, bf16[256,1280]{1,0:T(8,128)(2,1)S(1)}, u32[]{:S(2)}, u32[]{:S(2)}) collective-permute-start(bf16[256,1280]{1,0:T(8,128)(2,1)S(1)} %collective-permute-done.4), channel_id=1, source_target_pairs={{0,1},{1,2},{2,3},{3,4},{4,5},{5,6},{6,7},{7,8},{8,9},{9,10},{10,1... | collective-permute-start | bytes 1966088 | tf_op jit(solution)/shard_map/ppermute | solution.py:14
  62.6 1.2 fusion.45
  64.6 1.2 fusion.31
  69.0 6.0 %collective-permute-done.5 = bf16[256,1280]{1,0:T(8,128)(2,1)S(1)} collective-permute-done((bf16[256,1280]{1,0:T(8,128)(2,1)S(1)}, bf16[256,1280]{1,0:T(8,128)(2,1)S(1)}, u32[]{:S(2)}, u32[]{:S(2)}) %collective-permute-start.5) | collective-permute-done | bytes 655392 | tf_op jit(solution)/shard_map/ppermute | solution.py:14
  76.2 2.7 %collective-permute-start.6 = (bf16[256,1280]{1,0:T(8,128)(2,1)S(1)}, bf16[256,1280]{1,0:T(8,128)(2,1)S(1)}, u32[]{:S(2)}, u32[]{:S(2)}) collective-permute-start(bf16[256,1280]{1,0:T(8,128)(2,1)S(1)} %collective-permute-done.5), channel_id=1, source_target_pairs={{0,1},{1,2},{2,3},{3,4},{4,5},{5,6},{6,7},{7,8},{8,9},{9,10},{10,1... | collective-permute-start | bytes 1966088 | tf_op jit(solution)/shard_map/ppermute | solution.py:14
  81.0 1.2 fusion.52
  83.0 1.2 fusion.24
  85.3 1.1 fusion.21
  87.4 6.0 %collective-permute-done.6 = bf16[256,1280]{1,0:T(8,128)(2,1)S(1)} collective-permute-done((bf16[256,1280]{1,0:T(8,128)(2,1)S(1)}, bf16[256,1280]{1,0:T(8,128)(2,1)S(1)}, u32[]{:S(2)}, u32[]{:S(2)}) %collective-permute-start.6) | collective-permute-done | bytes 655392 | tf_op jit(solution)/shard_map/ppermute | solution.py:14
  94.6 2.5 %collective-permute-start.7 = (bf16[256,1280]{1,0:T(8,128)(2,1)S(1)}, bf16[256,1280]{1,0:T(8,128)(2,1)S(1)}, u32[]{:S(2)}, u32[]{:S(2)}) collective-permute-start(bf16[256,1280]{1,0:T(8,128)(2,1)S(1)} %collective-permute-done.6), channel_id=1, source_target_pairs={{0,1},{1,2},{2,3},{3,4},{4,5},{5,6},{6,7},{7,8},{8,9},{9,10},{10,1... | collective-permute-start | bytes 1966088 | tf_op jit(solution)/shard_map/ppermute | solution.py:14
  99.2 1.2 fusion.58
  101.2 1.2 fusion.17
  102.4 9.3 %collective-permute-done.7 = bf16[256,1280]{1,0:T(8,128)(2,1)S(1)} collective-permute-done((bf16[256,1280]{1,0:T(8,128)(2,1)S(1)}, bf16[256,1280]{1,0:T(8,128)(2,1)S(1)}, u32[]{:S(2)}, u32[]{:S(2)}) %collective-permute-start.7) | collective-permute-done | bytes 655392 | tf_op jit(solution)/shard_map/ppermute | solution.py:14
  114.9 1.2 fusion.64
  116.4 1.2 convolution_select_fusion
  118.0 1.4 %fusion.14 = f32[256,4352]{1,0:T(8,128)S(1)} fusion(f32[256,4352]{1,0:T(8,128)S(1)} %scatter-add.196, f32[256,2304]{1,0:T(8,128)S(1)} %fusion.76, pred[]{:T(512)} %compare_reduce_fusion.6, bf16[256,2304]{1,0:T(8,128)(2,1)S(1)} %multiply_convert_fusion.8), kind=kOutput, calls=%fused_computation.23 | convolution fusion | flops 304349184 | bytes 7208961 | tf_op jit(solution)/shard_map/dot_general | solution.py:46
  119.4 1.5 %fusion.12 = f32[256,4352]{1,0:T(8,128)S(1)} fusion(f32[256,4352]{1,0:T(8,128)S(1)} %fusion.14, f32[256,2304]{1,0:T(8,128)S(1)} %fusion.50, pred[]{:T(512)} %compare_reduce_fusion.5, bf16[256,2304]{1,0:T(8,128)(2,1)S(1)} %multiply_convert_fusion.8), kind=kOutput, calls=%fused_computation.20 | convolution fusion | flops 304349184 | bytes 7208961 | tf_op jit(solution)/shard_map/dot_general | solution.py:46
  120.9 1.5 %fusion.10 = f32[256,4352]{1,0:T(8,128)S(1)} fusion(f32[256,4352]{1,0:T(8,128)S(1)} %fusion.12, f32[256,2304]{1,0:T(8,128)S(1)} %fusion.43, pred[]{:T(512)} %compare_reduce_fusion.4, bf16[256,2304]{1,0:T(8,128)(2,1)S(1)} %multiply_convert_fusion.8), kind=kOutput, calls=%fused_computation.17 | convolution fusion | flops 304349184 | bytes 7208961 | tf_op jit(solution)/shard_map/dot_general | solution.py:46
  122.4 1.4 %fusion.8 = f32[256,4352]{1,0:T(8,128)S(1)} fusion(f32[256,4352]{1,0:T(8,128)S(1)} %fusion.10, bf16[256,2304]{1,0:T(8,128)(2,1)S(1)} %multiply_convert_fusion.8, pred[]{:T(512)} %compare_reduce_fusion.3), kind=kOutput, calls=%fused_computation.14 | convolution fusion | flops 303169536 | bytes 6029313 | tf_op jit(solution)/shard_map/dot_general | solution.py:46
  123.8 1.5 %fusion.6 = f32[256,4352]{1,0:T(8,128)S(1)} fusion(f32[256,4352]{1,0:T(8,128)S(1)} %fusion.8, f32[256,2304]{1,0:T(8,128)S(1)} %fusion.36, pred[]{:T(512)} %compare_reduce_fusion.2, bf16[256,2304]{1,0:T(8,128)(2,1)S(1)} %multiply_convert_fusion.8), kind=kOutput, calls=%fused_computation.11 | convolution fusion | flops 304349184 | bytes 7208961 | tf_op jit(solution)/shard_map/dot_general | solution.py:46
  125.3 1.4 %fusion.4 = f32[256,4352]{1,0:T(8,128)S(1)} fusion(f32[256,4352]{1,0:T(8,128)S(1)} %fusion.6, f32[256,2304]{1,0:T(8,128)S(1)} %fusion.29, pred[]{:T(512)} %compare_reduce_fusion.1, bf16[256,2304]{1,0:T(8,128)(2,1)S(1)} %multiply_convert_fusion.8), kind=kOutput, calls=%fused_computation.8 | convolution fusion | flops 304349184 | bytes 7208961 | tf_op jit(solution)/shard_map/dot_general | solution.py:46
  126.7 1.6 %fusion.2 = f32[256,4352]{1,0:T(8,128)S(1)} fusion(f32[256,4352]{1,0:T(8,128)S(1)} %fusion.4, f32[256,2304]{1,0:T(8,128)S(1)} %fusion.22, pred[]{:T(512)} %compare_reduce_fusion, bf16[256,2304]{1,0:T(8,128)(2,1)S(1)} %multiply_convert_fusion.8), kind=kOutput, calls=%fused_computation.5 | convolution fusion | flops 304349184 | bytes 7208961 | tf_op jit(solution)/shard_map/dot_general | solution.py:46
  129.4 2.4 %broadcast_multiply_fusion = f32[256,4352]{1,0:T(8,128)} fusion(f32[256,4352]{1,0:T(8,128)S(1)} %fusion), kind=kLoop, calls=%fused_computation.137 | loop fusion | flops 1114112 | bytes 8912896 | tf_op jit(solution)/shard_map/mul | solution.py:52
  (70 shorter events, 40.0 us)
Async XLA Ops:
  1.9 17.2 %collective-permute-start = (bf16[256,1280]{1,0:T(8,128)(2,1)S(1)}, bf16[256,1280]{1,0:T(8,128)(2,1)S(1)}, u32[]{:S(2)}, u32[]{:S(2)}) collective-permute-start(bf16[256,1280]{1,0:T(8,128)(2,1)S(1)} %fusion.81), channel_id=1, source_target_pairs={{0,1},{1,2},{2,3},{3,4},{4,5},{5,6},{6,7},{7,8},{8,9},{9,10},{10,1... | collective-permute-start | bytes 1966088 | tf_op jit(solution)/shard_map/ppermute | solution.py:14
  4.5 17.0 %collective-permute-start.2 = (bf16[256,1280]{1,0:T(8,128)(2,1)S(1)}, bf16[256,1280]{1,0:T(8,128)(2,1)S(1)}, u32[]{:S(2)}, u32[]{:S(2)}) collective-permute-start(bf16[256,1280]{1,0:T(8,128)(2,1)S(1)} %fusion.81), channel_id=1, source_target_pairs={{0,31},{1,0},{2,1},{3,2},{4,3},{5,4},{6,5},{7,6},{8,7},{9,8},{10,9... | collective-permute-start | bytes 1966088 | tf_op jit(solution)/shard_map/ppermute | solution.py:14
  19.1 17.0 %collective-permute-start.1 = (bf16[256,1280]{1,0:T(8,128)(2,1)S(1)}, bf16[256,1280]{1,0:T(8,128)(2,1)S(1)}, u32[]{:S(2)}, u32[]{:S(2)}) collective-permute-start(bf16[256,1280]{1,0:T(8,128)(2,1)S(1)} %collective-permute-done), channel_id=1, source_target_pairs={{0,1},{1,2},{2,3},{3,4},{4,5},{5,6},{6,7},{7,8},{8,9},{9,10},{10,1... | collective-permute-start | bytes 1966088 | tf_op jit(solution)/shard_map/ppermute | solution.py:14
  22.7 16.7 %collective-permute-start.3 = (bf16[256,1280]{1,0:T(8,128)(2,1)S(1)}, bf16[256,1280]{1,0:T(8,128)(2,1)S(1)}, u32[]{:S(2)}, u32[]{:S(2)}) collective-permute-start(bf16[256,1280]{1,0:T(8,128)(2,1)S(1)} %collective-permute-done.2), channel_id=1, source_target_pairs={{0,31},{1,0},{2,1},{3,2},{4,3},{5,4},{6,5},{7,6},{8,7},{9,8},{10,9... | collective-permute-start | bytes 1966088 | tf_op jit(solution)/shard_map/ppermute | solution.py:14
  40.5 16.3 %collective-permute-start.4 = (bf16[256,1280]{1,0:T(8,128)(2,1)S(1)}, bf16[256,1280]{1,0:T(8,128)(2,1)S(1)}, u32[]{:S(2)}, u32[]{:S(2)}) collective-permute-start(bf16[256,1280]{1,0:T(8,128)(2,1)S(1)} %collective-permute-done.1), channel_id=1, source_target_pairs={{0,1},{1,2},{2,3},{3,4},{4,5},{5,6},{6,7},{7,8},{8,9},{9,10},{10,1... | collective-permute-start | bytes 1966088 | tf_op jit(solution)/shard_map/ppermute | solution.py:14
  43.0 21.1 %collective-permute-start.8 = (bf16[256,1280]{1,0:T(8,128)(2,1)S(1)}, bf16[256,1280]{1,0:T(8,128)(2,1)S(1)}, u32[]{:S(2)}, u32[]{:S(2)}) collective-permute-start(bf16[256,1280]{1,0:T(8,128)(2,1)S(1)} %collective-permute-done.3), channel_id=1, source_target_pairs={{0,31},{1,0},{2,1},{3,2},{4,3},{5,4},{6,5},{7,6},{8,7},{9,8},{10,9... | collective-permute-start | bytes 1966088 | tf_op jit(solution)/shard_map/ppermute | solution.py:14
  57.9 17.1 %collective-permute-start.5 = (bf16[256,1280]{1,0:T(8,128)(2,1)S(1)}, bf16[256,1280]{1,0:T(8,128)(2,1)S(1)}, u32[]{:S(2)}, u32[]{:S(2)}) collective-permute-start(bf16[256,1280]{1,0:T(8,128)(2,1)S(1)} %collective-permute-done.4), channel_id=1, source_target_pairs={{0,1},{1,2},{2,3},{3,4},{4,5},{5,6},{6,7},{7,8},{8,9},{9,10},{10,1... | collective-permute-start | bytes 1966088 | tf_op jit(solution)/shard_map/ppermute | solution.py:14
  64.1 18.4 %collective-permute-start.9 = (bf16[256,1280]{1,0:T(8,128)(2,1)S(1)}, bf16[256,1280]{1,0:T(8,128)(2,1)S(1)}, u32[]{:S(2)}, u32[]{:S(2)}) collective-permute-start(bf16[256,1280]{1,0:T(8,128)(2,1)S(1)} %collective-permute-done.8), channel_id=1, source_target_pairs={{0,31},{1,0},{2,1},{3,2},{4,3},{5,4},{6,5},{7,6},{8,7},{9,8},{10,9... | collective-permute-start | bytes 1966088 | tf_op jit(solution)/shard_map/ppermute | solution.py:14
  76.2 17.3 %collective-permute-start.6 = (bf16[256,1280]{1,0:T(8,128)(2,1)S(1)}, bf16[256,1280]{1,0:T(8,128)(2,1)S(1)}, u32[]{:S(2)}, u32[]{:S(2)}) collective-permute-start(bf16[256,1280]{1,0:T(8,128)(2,1)S(1)} %collective-permute-done.5), channel_id=1, source_target_pairs={{0,1},{1,2},{2,3},{3,4},{4,5},{5,6},{6,7},{7,8},{8,9},{9,10},{10,1... | collective-permute-start | bytes 1966088 | tf_op jit(solution)/shard_map/ppermute | solution.py:14
  82.5 18.2 %collective-permute-start.10 = (bf16[256,1280]{1,0:T(8,128)(2,1)S(1)}, bf16[256,1280]{1,0:T(8,128)(2,1)S(1)}, u32[]{:S(2)}, u32[]{:S(2)}) collective-permute-start(bf16[256,1280]{1,0:T(8,128)(2,1)S(1)} %collective-permute-done.9), channel_id=1, source_target_pairs={{0,31},{1,0},{2,1},{3,2},{4,3},{5,4},{6,5},{7,6},{8,7},{9,8},{10,9... | collective-permute-start | bytes 1966088 | tf_op jit(solution)/shard_map/ppermute | solution.py:14
  94.6 17.1 %collective-permute-start.7 = (bf16[256,1280]{1,0:T(8,128)(2,1)S(1)}, bf16[256,1280]{1,0:T(8,128)(2,1)S(1)}, u32[]{:S(2)}, u32[]{:S(2)}) collective-permute-start(bf16[256,1280]{1,0:T(8,128)(2,1)S(1)} %collective-permute-done.6), channel_id=1, source_target_pairs={{0,1},{1,2},{2,3},{3,4},{4,5},{5,6},{6,7},{7,8},{8,9},{9,10},{10,1... | collective-permute-start | bytes 1966088 | tf_op jit(solution)/shard_map/ppermute | solution.py:14
  100.8 27.5 %collective-permute-start.11 = (bf16[256,1280]{1,0:T(8,128)(2,1)S(1)}, bf16[256,1280]{1,0:T(8,128)(2,1)S(1)}, u32[]{:S(2)}, u32[]{:S(2)}) collective-permute-start(bf16[256,1280]{1,0:T(8,128)(2,1)S(1)} %collective-permute-done.10), channel_id=1, source_target_pairs={{0,31},{1,0},{2,1},{3,2},{4,3},{5,4},{6,5},{7,6},{8,7},{9,8},{10,9... | collective-permute-start | bytes 1966088 | tf_op jit(solution)/shard_map/ppermute | solution.py:14
where the time goes:
time: 132 us
  matrix products  53.5 us (41%)
  waiting for transfers between devices  48.4 us (37%)
  starting transfers between devices  15.7 us (12%)
  other arithmetic  11.9 us (9%)
  local copies, waits for them, and re-layouts  1.68 us (1%)
    dot_general x54, matrix products, combine(): jnp.dot(block_rows[:, begin_col:begin_col + row_count], neighbour, prefer...  53.5 us
    ppermute x12, waiting for transfers between devices, shifted(): return lax.ppermute(value, axis, pairs)  48.4 us
    ppermute x12, starting transfers between devices, shifted(): return lax.ppermute(value, axis, pairs)  15.7 us
    another operation x11, other arithmetic  7.41 us
  transfers between devices with their start and end apart: 12, of which 6 were waited for; matrix products, arithmetic and copies ran while one was open for 46% of the time, Pallas kernels for 0%

commit v1 on v0

v1 whole, which is shorter than its diff:
```python
import functools
import math

import jax
import jax.numpy as jnp
from jax import lax
from jax.experimental import pallas as pl
from jax.experimental.pallas import tpu as pltpu
from jax.sharding import PartitionSpec as P

B = 512
MESH = pl.DeviceIdType.MESH
CORES = 2
PLANE = 4
SPAN = PLANE - 1
PAD = 16
CHUNKS = 4


def banded(adjacency, weight):
    row_count = adjacency.shape[0]
    reach = (adjacency.shape[1] // row_count - 1) // 2
    local_row = lax.broadcasted_iota(jnp.int32, adjacency.shape, 0)
    offset = lax.broadcasted_iota(jnp.int32, adjacency.shape, 1) - local_row - reach * row_count
    keep = (jnp.abs(offset) <= B) & ((adjacency == 1) | (offset == 0))
    return jnp.where(keep, weight, jnp.zeros_like(weight))


def pack(matrix):
    rows = matrix.shape[0]
    first, last = matrix[:, :rows], matrix[:, -rows:]
    r = lax.broadcasted_iota(jnp.int32, (rows, rows), 0)
    c = lax.broadcasted_iota(jnp.int32, (rows, rows), 1)
    square = jnp.where(c >= r, first, last)
    diagonal = jnp.sum(jnp.where(c == r, last, 0).astype(jnp.float32), axis=0, keepdims=True)
    diagonal = jnp.pad(diagonal.astype(matrix.dtype), ((0, PAD - 1), (0, matrix.shape[1] - 2 * rows)))
    body = jnp.concatenate([square, matrix[:, rows:-rows]], axis=1)
    return jnp.concatenate([body, diagonal], axis=0)


def kernel(
    n, rows, packed, out, buf, first, last, p_acc, t_acc, p_low, t_low,
    own_send, pair_send, hop_send, recv, local_sem,
):
    me = lax.axis_index("blk")
    core = me % CORES
    place = (me // CORES) % PLANE
    group = me // (CORES * PLANE)
    groups = n // (CORES * PLANE)
    partner = me + 1 - 2 * core
    up = ((group + 1) % groups * PLANE + place) * CORES + core
    down = ((group + groups - 1) % groups * PLANE + place) * CORES + core
    mates = (SPAN - place, (place + 2) % PLANE, place + 1 - 2 * (place % 2))

    def device(q):
        return (group * PLANE + q) * CORES + core

    def slot(chip_offset, c):
        return (chip_offset + SPAN) * CORES + c

    total = rows + PAD
    step = rows // CHUNKS
    bounds = [(j * step, step if j < CHUNKS - 1 else total - j * step) for j in range(CHUNKS)]

    barrier = pltpu.get_barrier_semaphore()
    greeted = [partner, up, down] + [device(q) for q in mates]
    for other in greeted:
        pl.semaphore_signal(barrier, inc=1, device_id=(other,), device_id_type=MESH)
    pl.semaphore_wait(barrier, len(greeted))

    def chunk(ref, j):
        return ref.at[pl.ds(bounds[j][0], bounds[j][1])]

    def own(index, j, to, at):
        return pltpu.make_async_remote_copy(
            src_ref=chunk(packed, j),
            dst_ref=chunk(buf.at[at], j),
            send_sem=own_send.at[index, j],
            recv_sem=recv.at[at, j],
            device_id=(to,),
            device_id_type=MESH,
        )

    def forward(sem, source, j, to, at):
        return pltpu.make_async_remote_copy(
            src_ref=chunk(buf.at[source], j),
            dst_ref=chunk(buf.at[at], j),
            send_sem=sem,
            recv_sem=recv.at[at, j],
            device_id=(to,),
            device_id_type=MESH,
        )

    def arrived(at, j):
        pltpu.make_async_copy(chunk(packed, j), chunk(buf.at[at], j), recv.at[at, j]).wait()

    sent = []

    def go(copy):
        copy.start()
        sent.append(copy)

    for j in range(CHUNKS):
        for index in (0, 1):
            go(own(index, j, device(mates[index]), slot(place - mates[index], core)))
    for j in range(CHUNKS):
        go(own(2, j, device(mates[2]), slot(place - mates[2], core)))
        go(own(3, j, partner, slot(0, core)))
    mine = pltpu.make_async_copy(packed, buf.at[slot(0, core)], local_sem)
    mine.start()
    p_acc[...] = jnp.zeros_like(p_acc)
    t_acc[...] = jnp.zeros_like(t_acc)
    out[...] = jnp.zeros_like(out)

    def mate_in(index, j):
        q = mates[index]
        at = slot(q - place, core)
        arrived(at, j)
        above = (q - place + PLANE) // PLANE
        target = above * up + (1 - above) * down
        there = slot(q - place + PLANE - 2 * PLANE * above, core)
        go(forward(hop_send.at[index, j], at, j, target, there))
        go(forward(pair_send.at[index, j], at, j, partner, at))

    def relay_slot(index, c):
        q = mates[index]
        above = (q - place + PLANE) // PLANE
        return slot(q - place + PLANE - 2 * PLANE * above, c)

    def relay_in(index, j):
        at = relay_slot(index, core)
        arrived(at, j)
        go(forward(pair_send.at[3 + index, j], at, j, partner, at))

    def other_in(at):
        for j in range(CHUNKS):
            arrived(at, j)

    def unpack(at):
        square = buf[at, :rows, :rows]
        r = lax.broadcasted_iota(jnp.int32, (rows, rows), 0)
        c = lax.broadcasted_iota(jnp.int32, (rows, rows), 1)
        diagonal = buf[at, rows : rows + 1, :rows]
        zero = jnp.zeros_like(square)
        first[at] = jnp.where(c >= r, square, zero)
        last[at] = jnp.where(c < r, square, jnp.where(c == r, diagonal, zero))

    middle = 3 * rows

    def unit(left, at, acc, column):
        begin = pl.multiple_of(column * rows, rows)
        for ref, start, width in (
            (first.at[at], 0, rows),
            (buf.at[at, pl.ds(0, rows), pl.ds(rows, middle)], rows, middle),
            (last.at[at], rows + middle, rows),
        ):
            where = pl.ds(pl.multiple_of(begin + start, rows), width)
            acc[:, where] += jnp.dot(left, ref[...], preferred_element_type=jnp.float32)

    for j in range(CHUNKS):
        mate_in(0, j)
        mate_in(1, j)
    for j in range(CHUNKS):
        mate_in(2, j)
        relay_in(0, j)
        relay_in(1, j)
    mine.wait()
    other_in(slot(0, 1 - core))
    for index in range(3):
        other_in(slot(mates[index] - place, 1 - core))
    for index in (0, 1):
        other_in(relay_slot(index, 1 - core))
    for j in range(CHUNKS):
        relay_in(2, j)
    other_in(relay_slot(2, 1 - core))

    def unpack_all(b, carry):
        unpack(b)
        return carry

    lax.fori_loop(0, (2 * SPAN + 1) * CORES, unpack_all, 0)

    center = slot(0, core)
    lefts = (
        [first[center]]
        + [buf[center, :rows, (1 + m) * rows : (2 + m) * rows] for m in range(3)]
        + [last[center]]
    )
    for t in range(5):
        unit(lefts[t], center - 2 + t, p_acc, t)
    p_low[...] = (p_acc[...] * (1.0 / math.sqrt(B))).astype(p_low.dtype)

    def second(t, carry):
        left = p_low[:, pl.ds(pl.multiple_of(t * rows, rows), rows)]
        unit(left, center - 4 + t, t_acc, t)
        return carry

    lax.fori_loop(0, 9, second, 0)
    scale = 1.0 / math.sqrt(B) / math.sqrt(2 * B)
    t_low[...] = (t_acc[...] * scale).astype(t_low.dtype)

    def third(t, carry):
        left = t_low[:, pl.ds(pl.multiple_of(t * rows, rows), rows)]
        unit(left, center - 6 + t, out, t)
        return carry

    lax.fori_loop(0, 13, third, 0)
    for copy in sent:
        copy.wait_send()


def local(n, adjacency, weight):
    rows = adjacency.shape[0]
    packed = pack(banded(adjacency, weight))
    wide = packed.shape[1]
    slots = (2 * SPAN + 1) * CORES
    low = packed.dtype
    return pl.pallas_call(
        functools.partial(kernel, n, rows),
        out_shape=jax.ShapeDtypeStruct((rows, 17 * rows), jnp.float32),
        in_specs=[pl.BlockSpec(memory_space=pltpu.VMEM)],
        out_specs=pl.BlockSpec(memory_space=pltpu.VMEM),
        scratch_shapes=[
            pltpu.VMEM((slots, rows + PAD, wide), low),
            pltpu.VMEM((slots, rows, rows), low),
            pltpu.VMEM((slots, rows, rows), low),
            pltpu.VMEM((rows, 9 * rows), jnp.float32),
            pltpu.VMEM((rows, 13 * rows), jnp.float32),
            pltpu.VMEM((rows, 9 * rows), low),
            pltpu.VMEM((rows, 13 * rows), low),
            pltpu.SemaphoreType.DMA((4, CHUNKS)),
            pltpu.SemaphoreType.DMA((6, CHUNKS)),
            pltpu.SemaphoreType.DMA((3, CHUNKS)),
            pltpu.SemaphoreType.DMA((slots, CHUNKS)),
            pltpu.SemaphoreType.DMA,
        ],
        compiler_params=pltpu.CompilerParams(
            collective_id=0, has_side_effects=True, vmem_limit_bytes=56 * 1024 * 1024
        ),
    )(packed)


def solution(mesh):
    in_specs = (P("blk", None), P("blk", None))
    out_specs = P("blk", None)
    n = mesh.shape["blk"]
    return jax.shard_map(
        functools.partial(local, n), mesh=mesh, in_specs=in_specs, out_specs=out_specs, check_vma=False
    )
```

time: 132 us -> 79.6 us (0.60)
  Pallas kernels: 0 us -> 71.9 us
  matrix products: 53.5 us -> 0 us
  waiting for transfers between devices: 48.4 us -> 0 us
  starting transfers between devices: 15.7 us -> 0 us
  other arithmetic: 11.9 us -> 2.8 us
  local copies, waits for them, and re-layouts: 1.68 us -> 4.68 us
    pallas_call x0 -> x1, Pallas kernels: none -> 71.9 us  [local(): pl.pallas_call(functools.partial(kernel, n, rows), out_shape=jax.ShapeDty...]
    dot_general x54 -> x0, matrix products: 53.5 us -> none  [combine(): jnp.dot(block_rows[:, begin_col:begin_col + row_count], neighbour, prefer...]
    ppermute x12 -> x0, waiting for transfers between devices: 48.4 us -> none  [shifted(): return lax.ppermute(value, axis, pairs)]
    ppermute x12 -> x0, starting transfers between devices: 15.7 us -> none  [shifted(): return lax.ppermute(value, axis, pairs)]
    another operation x11 -> x0, other arithmetic: 7.41 us -> none
    unnamed x0 -> x1, local copies, waits for them, and re-layouts: none -> 4.65 us
    mul x1 -> x0, other arithmetic: 2.39 us -> none  [combine(): return result * scale]
    scatter-add x10 -> x0, local copies, waits for them, and re-layouts: 1.68 us -> none  [combine(): result = result.at[:, begin_col:begin_col + width_cols].add(product)]
  transfers between devices with their start and end apart: 12 -> 0, of which waited for: 6 -> 0; matrix products, arithmetic and copies ran while one was open for 46% -> 0% of each run, Pallas kernels for 0% -> 0%
where the time goes in v1:
time: 79.6 us; the launch traced here: 79.4 us
  Pallas kernels  71.9 us (90%)
  local copies, waits for them, and re-layouts  4.68 us (6%)
  other arithmetic  2.8 us (4%)
    pallas_call x1, Pallas kernels, local(): pl.pallas_call(functools.partial(kernel, n, rows), out_shape=jax.ShapeDty...  71.9 us
    unnamed x1, local copies, waits for them, and re-layouts  4.65 us
    select_n x1, other arithmetic, banded(): return jnp.where(keep, weight, jnp.zeros_like(weight))  1.87 us

profile of v1, /device:TPU:1, one launch (start us, length us, event | category | flops | bytes accessed | tf_op | source)
XLA Modules:
  0.0 79.4 jit_solution(10971294004887848957)
XLA Ops:
  0.0 1.9 %fusion.3 = bf16[256,1280]{1,0:T(8,128)(2,1)S(1)} fusion(bf16[256,1280]{1,0:T(8,128)(2,1)} %param.3, s32[256,1280]{1,0:T(8,128)} %param.2), kind=kLoop, calls=%fused_computation.5 | loop fusion | flops 2949120 | bytes 2621440 | tf_op jit(solution)/shard_map/jit(_where)/select_n | solution.py:26
  1.9 0.1 fusion.6
  2.0 0.9 %fusion.5.packed = bf16[272,1024]{1,0:T(8,128)(2,1)} fusion(bf16[1,256]{1,0:T(2,128)(2,1)S(1)} %convert_element_type.17, bf16[256,768]{1,0:T(8,128)(2,1)S(1)} %slice.14, bf16[256,256]{1,0:T(8,128)(2,1)S(1)} %get-tuple-element.5), kind=kLoop, calls=%fused_computation.8 | loop fusion | flops 2228224 | bytes 1081856 | tf_op jit(solution)/shard_map/concatenate | solution.py:38
  2.9 71.9 %shard_map.28 = f32[256,4352]{1,0:T(8,128)} custom-call(bf16[272,1024]{1,0:T(8,128)(2,1)} %fusion.5.packed), custom_call_target="tpu_custom_call" | custom-call | tf_op jit(solution)/shard_map/pallas_call | solution.py:218
  74.8 4.6 %copy.4 = f32[256,4352]{1,0:T(8,128)} copy(f32[256,4352]{1,0:T(8,128)} %shard_map.28) | data formatting | bytes 8912896
  (2 shorter events, 0.0 us)

commit v2 on v1

v2 whole, which is shorter than its diff:
```python
import functools
import math

import jax
import jax.numpy as jnp
from jax import lax
from jax.experimental import pallas as pl
from jax.experimental.pallas import tpu as pltpu
from jax.sharding import PartitionSpec as P

B = 512
MESH = pl.DeviceIdType.MESH
CORES = 2
PLANE = 4
SPAN = PLANE - 1
PAD = 16
CHUNKS = 4


def banded(adjacency, weight):
    row_count = adjacency.shape[0]
    reach = (adjacency.shape[1] // row_count - 1) // 2
    local_row = lax.broadcasted_iota(jnp.int32, adjacency.shape, 0)
    offset = lax.broadcasted_iota(jnp.int32, adjacency.shape, 1) - local_row - reach * row_count
    keep = (jnp.abs(offset) <= B) & ((adjacency == 1) | (offset == 0))
    return jnp.where(keep, weight, jnp.zeros_like(weight))


def pack(matrix):
    rows = matrix.shape[0]
    first, last = matrix[:, :rows], matrix[:, -rows:]
    r = lax.broadcasted_iota(jnp.int32, (rows, rows), 0)
    c = lax.broadcasted_iota(jnp.int32, (rows, rows), 1)
    square = jnp.where(c >= r, first, last)
    diagonal = jnp.sum(jnp.where(c == r, last, 0).astype(jnp.float32), axis=0, keepdims=True)
    diagonal = jnp.pad(diagonal.astype(matrix.dtype), ((0, PAD - 1), (0, matrix.shape[1] - 2 * rows)))
    body = jnp.concatenate([square, matrix[:, rows:-rows]], axis=1)
    return jnp.concatenate([body, diagonal], axis=0)


def kernel(
    n, rows, packed, out, buf, cols, row, p_low, t_low,
    own_send, pair_send, hop_send, side_send, recv, local_sem,
):
    me = lax.axis_index("blk")
    core = me % CORES
    place = (me // CORES) % PLANE
    group = me // (CORES * PLANE)
    groups = n // (CORES * PLANE)
    partner = me + 1 - 2 * core
    up = ((group + 1) % groups * PLANE + place) * CORES + core
    down = ((group + groups - 1) % groups * PLANE + place) * CORES + core
    x_mate = place + 1 - 2 * (place % 2)
    y_mate = (place + 2) % PLANE
    inner = (place + 1) // 2 % 2
    a_mate = (1 - inner) * x_mate + inner * y_mate
    b_mate = inner * x_mate + (1 - inner) * y_mate
    d_mate = SPAN - place

    def device(q):
        return (group * PLANE + q) * CORES + core

    def slot(chip_offset, c):
        return (chip_offset + SPAN) * CORES + c

    def is_above(q, p):
        return (q - p + PLANE) // PLANE

    def cross(q, p):
        return q - p + PLANE - 2 * PLANE * is_above(q, p)

    total = rows + PAD
    step = rows // CHUNKS
    bounds = [(j * step, step if j < CHUNKS - 1 else total - j * step) for j in range(CHUNKS)]

    barrier = pltpu.get_barrier_semaphore()
    greeted = [partner, up, down, device(a_mate), device(b_mate)]
    for other in greeted:
        pl.semaphore_signal(barrier, inc=1, device_id=(other,), device_id_type=MESH)
    pl.semaphore_wait(barrier, len(greeted))

    def chunk(ref, j):
        return ref.at[pl.ds(bounds[j][0], bounds[j][1])]

    sent = []

    def send(source, sem, j, to, at):
        copy = pltpu.make_async_remote_copy(
            src_ref=chunk(source, j),
            dst_ref=chunk(buf.at[at], j),
            send_sem=sem,
            recv_sem=recv.at[at, j],
            device_id=(to,),
            device_id_type=MESH,
        )
        copy.start()
        sent.append(copy)

    def arrived(at, j):
        pltpu.make_async_copy(chunk(packed, j), chunk(buf.at[at], j), recv.at[at, j]).wait()

    def pair(index, at, j):
        send(buf.at[at], pair_send.at[index, j], j, partner, at)

    def hop(index, q, j):
        above = is_above(q, place)
        to = above * up + (1 - above) * down
        send(buf.at[slot(q - place, core)], hop_send.at[index, j], j, to, slot(cross(q, place), core))

    center = slot(0, core)
    a_in, b_in, d_in = (slot(q - place, core) for q in (a_mate, b_mate, d_mate))
    a_far, b_far, d_far = (slot(cross(q, place), core) for q in (a_mate, b_mate, d_mate))

    for j in range(CHUNKS):
        send(packed, own_send.at[0, j], j, device(b_mate), slot(place - b_mate, core))
        send(packed, own_send.at[1, j], j, device(a_mate), slot(place - a_mate, core))
    mine = pltpu.make_async_copy(packed, buf.at[center], local_sem)
    mine.start()
    for j in range(CHUNKS):
        send(packed, own_send.at[2, j], j, partner, center)

    r = lax.broadcasted_iota(jnp.int32, (rows, rows), 0)
    c = lax.broadcasted_iota(jnp.int32, (rows, rows), 1)

    def triangles(at):
        square = buf[at, :rows, :rows]
        diagonal = buf[at, rows : rows + 1, :rows]
        zero = jnp.zeros_like(square)
        return (
            jnp.where(c >= r, square, zero),
            jnp.where(c < r, square, jnp.where(c == r, diagonal, zero)),
        )

    def unpack(at):
        first, last = triangles(at)
        cols[at, 4 * rows : 5 * rows, :] = first
        for k in range(1, 4):
            cols[at + k, (4 - k) * rows : (5 - k) * rows, :] = buf[at, :rows, k * rows : (k + 1) * rows]
        cols[at + 4, :rows, :] = last

    def take_other(at):
        other = at + 1 - 2 * core
        for j in range(CHUNKS):
            arrived(other, j)
        unpack(other)

    for j in range(CHUNKS):
        arrived(b_in, j)
        hop(0, b_mate, j)
        pair(0, b_in, j)
        arrived(a_in, j)
        send(buf.at[a_in], side_send.at[0, j], j, device(b_mate), slot(a_mate - b_mate, core))
        pair(1, a_in, j)
    for j in range(CHUNKS):
        hop(1, a_mate, j)
    for j in range(CHUNKS):
        arrived(b_far, j)
        send(
            buf.at[b_far], side_send.at[1, j], j, device(a_mate),
            slot(cross(b_mate, place) + place - a_mate, core),
        )
        pair(2, b_far, j)
    mine.wait()
    first, last = triangles(center)
    row[:, :rows] = first
    row[:, rows : 4 * rows] = buf[center, :rows, rows:]
    row[:, 4 * rows :] = last
    for at in (center, a_in, b_in, b_far):
        unpack(at)
    for at in (center, a_in, b_in):
        take_other(at)
    for j in range(CHUNKS):
        arrived(d_in, j)
        pair(3, d_in, j)
        arrived(a_far, j)
        pair(4, a_far, j)
        arrived(d_far, j)
        pair(5, d_far, j)
    for at in (d_in, a_far, d_far):
        unpack(at)
    for at in (b_far, d_in, a_far, d_far):
        take_other(at)

    def product(left, least, most, column):
        low, high = max(least, column - 4), min(most, column)
        return jnp.dot(
            left[:, (low - least) * rows : (high + 1 - least) * rows],
            cols[column + core, (low - column + 4) * rows : (high - column + 5) * rows, :],
            preferred_element_type=jnp.float32,
        )

    for u in range(9):
        p_low[:, u * rows : (u + 1) * rows] = (
            product(row, 4, 8, u + 4) * (1.0 / math.sqrt(B))
        ).astype(p_low.dtype)
    scale = 1.0 / math.sqrt(B) / math.sqrt(2 * B)
    for u in range(13):
        t_low[:, u * rows : (u + 1) * rows] = (product(p_low, 2, 10, u + 2) * scale).astype(t_low.dtype)
    for u in range(17):
        out[:, u * rows : (u + 1) * rows] = product(t_low, 0, 12, u)
    for copy in sent:
        copy.wait_send()


def local(n, adjacency, weight):
    rows = adjacency.shape[0]
    packed = pack(banded(adjacency, weight))
    wide = packed.shape[1]
    slots = (2 * SPAN + 1) * CORES
    low = packed.dtype
    return pl.pallas_call(
        functools.partial(kernel, n, rows),
        out_shape=jax.ShapeDtypeStruct((rows, 17 * rows), jnp.float32),
        in_specs=[pl.BlockSpec(memory_space=pltpu.VMEM)],
        out_specs=pl.BlockSpec(memory_space=pltpu.VMEM),
        scratch_shapes=[
            pltpu.VMEM((slots, rows + PAD, wide), low),
            pltpu.VMEM((slots + 4, 5 * rows, rows), low),
            pltpu.VMEM((rows, 5 * rows), low),
            pltpu.VMEM((rows, 9 * rows), low),
            pltpu.VMEM((rows, 13 * rows), low),
            pltpu.SemaphoreType.DMA((3, CHUNKS)),
            pltpu.SemaphoreType.DMA((6, CHUNKS)),
            pltpu.SemaphoreType.DMA((2, CHUNKS)),
            pltpu.SemaphoreType.DMA((2, CHUNKS)),
            pltpu.SemaphoreType.DMA((slots, CHUNKS)),
            pltpu.SemaphoreType.DMA,
        ],
        compiler_params=pltpu.CompilerParams(
            collective_id=0, has_side_effects=True, vmem_limit_bytes=40 * 1024 * 1024
        ),
    )(packed)


def solution(mesh):
    in_specs = (P("blk", None), P("blk", None))
    out_specs = P("blk", None)
    n = mesh.shape["blk"]
    return jax.shard_map(
        functools.partial(local, n), mesh=mesh, in_specs=in_specs, out_specs=out_specs, check_vma=False
    )
```

time: 79.6 us -> 47.8 us (0.60)
  Pallas kernels: 71.9 us -> 43.5 us
  local copies, waits for them, and re-layouts: 4.68 us -> 2.13 us
  other arithmetic: 2.8 us -> 1.99 us
    pallas_call x1, Pallas kernels: 71.9 us -> 43.5 us  [local(): pl.pallas_call(functools.partial(kernel, n, rows), out_shape=jax.ShapeDty...]
    unnamed x1, local copies, waits for them, and re-layouts: 4.65 us -> 2.1 us
    concatenate x1, other arithmetic: 0.87 us -> 0.06 us  [pack(): return jnp.concatenate([body, diagonal], axis=0)]
where the time goes in v2:
time: 47.8 us; the launch traced here: 47.7 us
  Pallas kernels  43.5 us (91%)
  local copies, waits for them, and re-layouts  2.13 us (4%)
  other arithmetic  1.99 us (4%)
    pallas_call x1, Pallas kernels, local(): pl.pallas_call(functools.partial(kernel, n, rows), out_shape=jax.ShapeDty...  43.5 us
    unnamed x1, local copies, waits for them, and re-layouts  2.1 us
    select_n x1, other arithmetic, banded(): return jnp.where(keep, weight, jnp.zeros_like(weight))  1.87 us

profile of v2, /device:TPU:1, one launch (start us, length us, event | category | flops | bytes accessed | tf_op | source)
XLA Modules:
  0.0 47.7 jit_solution(1203398695016226088)
XLA Ops:
  0.0 1.9 %fusion.3 = bf16[256,1280]{1,0:T(8,128)(2,1)S(1)} fusion(bf16[256,1280]{1,0:T(8,128)(2,1)} %param.3, s32[256,1280]{1,0:T(8,128)} %param.2), kind=kLoop, calls=%fused_computation.5 | loop fusion | flops 2949120 | bytes 2621440 | tf_op jit(solution)/shard_map/jit(_where)/select_n | solution.py:26
  1.9 0.1 fusion.6
  2.0 0.1 fusion.5.packed
  2.0 43.5 %shard_map.28 = f32[256,4352]{1,0:T(8,128)S(1)} custom-call(bf16[272,1024]{1,0:T(8,128)(2,1)S(1)} %fusion.5.packed), custom_call_target="tpu_custom_call" | custom-call | tf_op jit(solution)/shard_map/pallas_call | solution.py:211
  45.6 2.1 %copy.4 = f32[256,4352]{1,0:T(8,128)} copy(f32[256,4352]{1,0:T(8,128)S(1)} %shard_map.28) | data formatting | bytes 8912896
  (2 shorter events, 0.0 us)
